TPU v7x, 256 devices: a whole 4x4x8 slice. The times are simulated.
256 devices in a mesh: row: 16 (over y, z_hi, core), col: 16 (over z_lo, x).
Axes of the slice: x: 4, y: 4, z: 8 (z_hi: 2, z_lo: 4; z = z_hi * 4 + z_lo), core: 2. Of those that a mesh axis runs over, the one named last changes fastest.
Arguments:
- fluid_data: float32 [51, 32768], P(None, ('row', 'col')), as said below
- center_data: float32 [51, 16384], P(None, ('col', 'row')), as said below
- poly_coef: float32 [48, 4], replicated, may hold values from -3 to 3
Outputs:
- fluid_motion: float32 [48, 32768], P(None, ('row', 'col'))
- center_load: float32 [48, 16384], P(None, ('col', 'row'))
Inputs may be any that keep to these rules, and one draw needn't show every extreme that they name: Rows 0 to 2 of fluid_data lie in [0, 1]; rows 3 and on are forces. Rows 0 and 1 of center_data lie in [0, 1] and row 2 lies in [-0.5, -0.02], so every center is at least 0.02 below every vertex; rows 3 and on are coefficients.
All inputs are finite; a program needn't handle non-finite values.
Results may differ from a plain program's by a relative error of at most 0.0003.
Values sent between devices are 32-bit elements; how exact they have to be, the bound alone decides.
No kernel may reach another device: no remote copies, remote signals or barrier semaphores. Data moves between devices by JAX's collectives and lax.ppermute only.
A program may use at most 64 MiB of HBM per device.

v0:
```python
import jax
import jax.numpy as jnp
from jax import lax
from jax.experimental import pallas as pl
from jax.experimental.pallas import tpu as pltpu
from jax.sharding import PartitionSpec as P


WAVES = 64
COLS = 48
LANES = 128
LEAD = 5.217319695266324
TAIL = (-2.2719599305658895, 2.482104102078497, -1.26081348824302, 0.1916653466086582)


def tile_values(cx, cy, cz, fx, fy, fz):
    dx = cx - fx
    dy = cy - fy
    dz = cz - fz
    sq = dx * dx + dy * dy + dz * dz
    inv = lax.rsqrt(sq)
    turns = sq * inv
    rest = turns - jnp.round(turns)
    z = rest * rest
    p = z + TAIL[0]
    for c in TAIL[1:]:
        p = p * z + c
    return (rest * inv) * p


def high(a):
    return a.astype(jnp.bfloat16).astype(jnp.float32)


def quad_body(nfl, nfirst, *refs):
    center = refs[0]
    fluids = refs[1:1 + nfl]
    n = 1 + nfl
    load_in = refs[n] if nfirst[0] else None
    n += nfirst[0]
    motion_in = refs[n] if nfirst[1] else None
    n += nfirst[1]
    load_out = refs[n]
    motion_outs = refs[n + 1:n + 1 + nfl]
    cpos, cval, fval, fpos, t0, t1, acc, loads = refs[n + 1 + nfl:]
    hf = fluids[0].shape[0]
    nf = nfl * hf
    nb = center.shape[0] // 2
    half = lax.broadcasted_iota(jnp.int32, (1, LANES), 1) < LANES // 2
    for k in range(nf):
        s = slice(k * LANES, (k + 1) * LANES)
        chunk = fluids[k // hf].at[k % hf]
        val = chunk[3:3 + COLS, :] * LEAD
        hi = high(val)
        fval[0:COLS, s] = hi
        fval[COLS:2 * COLS, s] = val - hi
        fpos[:, s] = chunk[0:3, :] * float(WAVES)
    for b in range(nb):
        one = center[2 * b]
        two = center[2 * b + 1]
        top = jnp.where(half, one, pltpu.roll(two, LANES // 2, 1))
        bot = jnp.where(half, pltpu.roll(one, LANES // 2, 1), two)
        val = jnp.concatenate([top[0:24], bot[0:24]], 0) * LEAD
        hi = high(val)
        v = jnp.concatenate([hi, val - hi], 0)
        cval[b, :, 0:LANES] = v
        cval[b, :, LANES:2 * LANES] = v
        pos = jnp.concatenate([top[24:26], bot[24:25], jnp.zeros((5, LANES), jnp.float32)], 0) * float(WAVES)
        post = jnp.transpose(pos)
        for a in range(3):
            cpos[a, b * LANES:(b + 1) * LANES, :] = jnp.broadcast_to(post[:, a:a + 1], (LANES, LANES))

    def compute(b, t):
        for k in range(nf):
            s = slice(k * LANES, (k + 1) * LANES)
            fx = fpos[0:1, s]
            fy = fpos[1:2, s]
            fz = fpos[2:3, s]
            for g in range(LANES // 8):
                rows = slice(b * LANES + g * 8, b * LANES + (g + 1) * 8)
                v = tile_values(cpos[0, rows, :], cpos[1, rows, :], cpos[2, rows, :], fx, fy, fz)
                t[g * 8:(g + 1) * 8, s] = v
                t[LANES + g * 8:LANES + (g + 1) * 8, s] = v - high(v)

    def dots(b, t):
        m = jnp.dot(cval[b], t[...], preferred_element_type=jnp.float32)
        if b == 0:
            acc[...] = m
        else:
            acc[...] += m
        back = lax.dot_general(t[...], fval[...], (((1,), (1,)), ((), ())), preferred_element_type=jnp.float32)
        loads[b * LANES:(b + 1) * LANES, :] = back[0:LANES, :] + back[LANES:2 * LANES, :]

    ts = (t0, t1)
    compute(0, t0)
    for b in range(nb):
        if b + 1 < nb:
            compute(b + 1, ts[(b + 1) % 2])
        dots(b, ts[b % 2])

    for k in range(nf):
        s = slice(k * LANES, (k + 1) * LANES)
        m = acc[0:COLS, s] + acc[COLS:2 * COLS, s]
        if motion_in is not None and k < hf:
            m = m + motion_in[k]
        motion_outs[k // hf][k % hf] = m
    for b in range(nb):
        l = jnp.transpose(loads[b * LANES:(b + 1) * LANES, :])
        l = l[0:COLS] + l[COLS:2 * COLS]
        top = l[0:24]
        bot = l[24:48]
        one = jnp.where(half, top, pltpu.roll(bot, LANES // 2, 1))
        two = jnp.where(half, pltpu.roll(top, LANES // 2, 1), bot)
        if load_in is not None:
            one = one + load_in[2 * b]
            two = two + load_in[2 * b + 1]
        load_out[2 * b] = one
        load_out[2 * b + 1] = two


def quad(center, fluids, load=None, motion=None):
    hf = fluids[0].shape[0]
    hc = center.shape[0]
    nb = hc // 2
    width = len(fluids) * hf * LANES
    extra = tuple(a for a in (load, motion) if a is not None)

    def body(*refs):
        quad_body(len(fluids), (load is not None, motion is not None), *refs)

    vm = pl.BlockSpec(memory_space=pltpu.VMEM)
    return pl.pallas_call(
        body,
        out_shape=(jax.ShapeDtypeStruct((hc, COLS // 2, LANES), jnp.float32),)
        + (jax.ShapeDtypeStruct((hf, COLS, LANES), jnp.float32),) * len(fluids),
        in_specs=[vm] * (1 + len(fluids) + len(extra)),
        out_specs=(vm,) * (1 + len(fluids)),
        scratch_shapes=[
            pltpu.VMEM((3, nb * LANES, LANES), jnp.float32),
            pltpu.VMEM((nb, 2 * COLS, 2 * LANES), jnp.float32),
            pltpu.VMEM((2 * COLS, width), jnp.float32),
            pltpu.VMEM((3, width), jnp.float32),
            pltpu.VMEM((2 * LANES, width), jnp.float32),
            pltpu.VMEM((2 * LANES, width), jnp.float32),
            pltpu.VMEM((2 * COLS, width), jnp.float32),
            pltpu.VMEM((nb * LANES, 2 * COLS), jnp.float32),
        ],
        compiler_params=pltpu.CompilerParams(vmem_limit_bytes=20 * 2**20),
    )(center, *fluids, *extra)


def pack_body(center, out):
    half = center.shape[1]
    out[0:24, 0:half] = center[3:27, :]
    out[0:24, half:] = center[27:51, :]
    out[24:26, 0:half] = center[0:2, :]
    out[24:25, half:] = center[2:3, :]
    out[25:26, half:] = jnp.zeros((1, half), jnp.float32)


def packed(center):
    return pl.pallas_call(
        pack_body,
        out_shape=jax.ShapeDtypeStruct((26, LANES), jnp.float32),
        in_specs=[pl.BlockSpec(memory_space=pltpu.VMEM)],
        out_specs=pl.BlockSpec(memory_space=pltpu.VMEM),
        compiler_params=pltpu.CompilerParams(vmem_limit_bytes=2**20),
        name="pack",
    )(center)


AXES = ("row", "col")


def place(x, y, z, core):
    return (y * 4 + (z // 4) * 2 + core) * 16 + (z % 4) * 4 + x


def partners(move):
    spots = [(x, y, z, c) for x in range(4) for y in range(4) for z in range(8) for c in range(2)]
    return [(place(*spot), place(*move(*spot))) for spot in spots]


def near(v):
    return v ^ 1


def wrap(v):
    return 3 - v


FLUID_STAGES = (
    partners(lambda x, y, z, c: (x, y, z ^ 2, c)),
    partners(lambda x, y, z, c: (near(x), y, z, c)),
    partners(lambda x, y, z, c: (wrap(x), y, z, c)),
    partners(lambda x, y, z, c: (x, y, z, 1 - c)),
)
CENTER_STAGES = (
    partners(lambda x, y, z, c: (x, y, z ^ 1, c)),
    partners(lambda x, y, z, c: (x, y, 2 * wrap(z // 2) + z % 2, c)),
    partners(lambda x, y, z, c: (x, near(y), z, c)),
    partners(lambda x, y, z, c: (x, wrap(y), z, c)),
)


def gather_step(held, stage):
    return held, lax.ppermute(held, AXES, stage)


def sum_step(mine, theirs, stage):
    arrived = lax.ppermute(theirs, AXES, stage)
    half = mine.shape[0] // 2
    return mine[:half] + arrived[:half], mine[half:] + arrived[half:]


def per_device(fluid_data, center_data, poly_coef):
    fluid = fluid_data[None]
    center = packed(center_data)[None]
    fluids = (fluid, None)
    centers = (center, None)
    for i in range(4):
        held = centers[0] if i == 0 else jnp.concatenate(centers, 0)
        centers = gather_step(held, CENTER_STAGES[i])
        held = fluids[0] if i == 0 else jnp.concatenate(fluids, 0)
        fluids = gather_step(held, FLUID_STAGES[i])
    loads, motion = quad(centers[0], fluids[:1])
    loads_away, motion, motion_away = quad(centers[1], fluids, motion=motion)
    loads, motion_away = quad(centers[0], fluids[1:], load=loads, motion=motion_away)
    for i in (3, 2, 1):
        loads, loads_away = sum_step(loads, loads_away, CENTER_STAGES[i])
        motion, motion_away = sum_step(motion, motion_away, FLUID_STAGES[i])
    loads = (loads + lax.ppermute(loads_away, AXES, CENTER_STAGES[0]))[0]
    motion = (motion + lax.ppermute(motion_away, AXES, FLUID_STAGES[0]))[0]
    affine = poly_coef[:, 0:1] + jnp.dot(
        poly_coef[:, 1:],
        fluid_data[:3],
        precision=lax.Precision.HIGHEST,
        preferred_element_type=jnp.float32,
    )
    half = center_data.shape[1]
    return (motion + affine, jnp.concatenate([loads[:, :half], loads[:, half:]], 0))


def solution(mesh):
    placed = (P(None, ("row", "col")), P(None, ("col", "row")), P())
    return jax.shard_map(
        per_device,
        mesh=mesh,
        in_specs=placed,
        out_specs=(P(None, ("row", "col")), P(None, ("col", "row"))),
        check_vma=False,
    )
```

profile of v0, /device:TPU:32, one launch (start us, length us, event | category | flops | bytes accessed | tf_op | source)
XLA Modules:
  0.0 63.8 jit_solution(4491785575263287768)
XLA Ops:
  0.6 3.4 %collective-permute-start.4 = (f32[1,51,128]{2,1,0:T(8,128)}, f32[1,51,128]{2,1,0:T(8,128)S(1)}, u32[]{:S(2)}, u32[]{:S(2)}) collective-permute-start(f32[1,51,128]{2,1,0:T(8,128)} %bitcast.14), channel_id=1, source_target_pairs={{0,8},{16,24},{4,12},{20,28},{8,0},{24,16},{12,4},{28,20},{32,40},... | collective-permute-start | bytes 78344 | tf_op jit(solution)/shard_map/ppermute | solution.py:207
  4.0 0.7 %copy-done = f32[51,64]{1,0:T(8,128)S(1)} copy-done((f32[51,64]{1,0:T(8,128)S(1)}, f32[51,64]{1,0:T(8,128)}, u32[]{:S(2)}) %copy-start) | copy-done | bytes 13080
  4.9 1.1 %collective-permute-done.4 = f32[1,51,128]{2,1,0:T(8,128)S(1)} collective-permute-done((f32[1,51,128]{2,1,0:T(8,128)}, f32[1,51,128]{2,1,0:T(8,128)S(1)}, u32[]{:S(2)}, u32[]{:S(2)}) %collective-permute-start.4) | collective-permute-done | bytes 26144 | tf_op jit(solution)/shard_map/ppermute | solution.py:207
  6.1 1.6 %collective-permute-start.5 = (f32[2,51,128]{2,1,0:T(8,128)S(1)}, f32[2,51,128]{2,1,0:T(8,128)S(1)}, u32[]{:S(2)}, u32[]{:S(2)}) collective-permute-start(f32[2,51,128]{2,1,0:T(8,128)S(1)} %pad_maximum_fusion.4), channel_id=1, source_target_pairs={{0,1},{16,17},{4,5},{20,21},{8,9},{24,25},{12,13},{28,29},{32,33},... | collective-permute-start | bytes 156680 | tf_op jit(solution)/shard_map/ppermute | solution.py:207
  7.6 0.9 %collective-permute-done = f32[1,26,128]{2,1,0:T(8,128)S(1)} collective-permute-done((f32[1,26,128]{2,1,0:T(8,128)S(1)}, f32[1,26,128]{2,1,0:T(8,128)S(1)}, u32[]{:S(2)}, u32[]{:S(2)}) %collective-permute-start) | collective-permute-done | bytes 13344 | tf_op jit(solution)/shard_map/ppermute | solution.py:207
  8.6 4.2 %collective-permute-start.1 = (f32[2,26,128]{2,1,0:T(8,128)S(1)}, f32[2,26,128]{2,1,0:T(8,128)S(1)}, u32[]{:S(2)}, u32[]{:S(2)}) collective-permute-start(f32[2,26,128]{2,1,0:T(8,128)S(1)} %pad_maximum_fusion.5), channel_id=1, source_target_pairs={{0,40},{16,56},{4,44},{20,60},{8,32},{24,48},{12,36},{28,52},{32,8... | collective-permute-start | bytes 79880 | tf_op jit(solution)/shard_map/ppermute | solution.py:207
  12.8 2.2 %collective-permute-start.6 = (f32[4,51,128]{2,1,0:T(8,128)S(1)}, f32[4,51,128]{2,1,0:T(8,128)S(1)}, u32[]{:S(2)}, u32[]{:S(2)}) collective-permute-start(f32[4,51,128]{2,1,0:T(8,128)S(1)} %pad_maximum_fusion.2), channel_id=1, source_target_pairs={{0,3},{16,19},{4,7},{20,23},{8,11},{24,27},{12,15},{28,31},{32,35}... | collective-permute-start | bytes 313352 | tf_op jit(solution)/shard_map/ppermute | solution.py:207
  15.0 1.7 %collective-permute-start.2 = (f32[4,26,128]{2,1,0:T(8,128)S(1)}, f32[4,26,128]{2,1,0:T(8,128)S(1)}, u32[]{:S(2)}, u32[]{:S(2)}) collective-permute-start(f32[4,26,128]{2,1,0:T(8,128)S(1)} %pad_maximum_fusion.3), channel_id=1, source_target_pairs={{0,64},{16,80},{4,68},{20,84},{8,72},{24,88},{12,76},{28,92},{32,9... | collective-permute-start | bytes 159752 | tf_op jit(solution)/shard_map/ppermute | solution.py:207
  16.7 2.2 %collective-permute-done.6 = f32[4,51,128]{2,1,0:T(8,128)S(1)} collective-permute-done((f32[4,51,128]{2,1,0:T(8,128)S(1)}, f32[4,51,128]{2,1,0:T(8,128)S(1)}, u32[]{:S(2)}, u32[]{:S(2)}) %collective-permute-start.6) | collective-permute-done | bytes 104480 | tf_op jit(solution)/shard_map/ppermute | solution.py:207
  19.4 3.1 %collective-permute-start.3 = (f32[8,26,128]{2,1,0:T(8,128)S(1)}, f32[8,26,128]{2,1,0:T(8,128)S(1)}, u32[]{:S(2)}, u32[]{:S(2)}) collective-permute-start(f32[8,26,128]{2,1,0:T(8,128)S(1)} %pad_maximum_fusion.1.refs_0_), channel_id=1, source_target_pairs={{0,192},{16,208},{4,196},{20,212},{8,200},{24,216},{12,204},{28,22... | collective-permute-start | bytes 319496 | tf_op jit(solution)/shard_map/ppermute | solution.py:207
  22.5 2.5 %shard_map.50 = (f32[8,24,128]{2,1,0:T(8,128)S(1)}, f32[8,48,128]{2,1,0:T(8,128)S(1)}) custom-call(f32[8,26,128]{2,1,0:T(8,128)S(1)} %pad_maximum_fusion.1.refs_0_, f32[8,51,128]{2,1,0:T(8,128)S(1)} %pad_maximum_fusion.refs_1_), custom_call_target="tpu_custom_call" | custom-call | tf_op jit(solution)/shard_map/pallas_call | solution.py:132
  25.0 1.2 %collective-permute-done.3.refs_0_ = f32[8,26,128]{2,1,0:T(8,128)S(1)} collective-permute-done((f32[8,26,128]{2,1,0:T(8,128)S(1)}, f32[8,26,128]{2,1,0:T(8,128)S(1)}, u32[]{:S(2)}, u32[]{:S(2)}) %collective-permute-start.3) | collective-permute-done | bytes 106528 | tf_op jit(solution)/shard_map/ppermute | solution.py:207
  26.3 4.6 %shard_map.51 = (f32[8,24,128]{2,1,0:T(8,128)S(1)}, f32[8,48,128]{2,1,0:T(8,128)S(1)}, f32[8,48,128]{2,1,0:T(8,128)S(1)}) custom-call(f32[8,26,128]{2,1,0:T(8,128)S(1)} %collective-permute-done.3.refs_0_, f32[8,51,128]{2,1,0:T(8,128)S(1)} %pad_maximum_fusion.refs_1_, f32[8,51,128]{2,1,0:T(8,128)S(1)} %collective-permute-done.7.refs_2_.refs_1_, ...), custom_call_target="tpu_custom_call" | custom-call | tf_op jit(solution)/shard_map/pallas_call | solution.py:132
  30.9 3.2 %collective-permute-start.12 = (f32[8,24,128]{2,1,0:T(8,128)S(1)}, f32[8,24,128]{2,1,0:T(8,128)S(1)}, u32[]{:S(2)}, u32[]{:S(2)}) collective-permute-start(f32[8,24,128]{2,1,0:T(8,128)S(1)} %get-tuple-element.15), channel_id=1, source_target_pairs={{0,192},{16,208},{4,196},{20,212},{8,200},{24,216},{12,204},{28,22... | collective-permute-start | bytes 294920 | tf_op jit(solution)/shard_map/ppermute | solution.py:211
  34.1 2.6 %shard_map.52 = (f32[8,24,128]{2,1,0:T(8,128)S(1)}, f32[8,48,128]{2,1,0:T(8,128)S(1)}) custom-call(f32[8,26,128]{2,1,0:T(8,128)S(1)} %pad_maximum_fusion.1.refs_0_, f32[8,51,128]{2,1,0:T(8,128)S(1)} %collective-permute-done.7.refs_2_.refs_1_, f32[8,24,128]{2,1,0:T(8,128)S(1)} %get-tuple-element.11.refs_2_, f32[8,48,128]{2,1,0:T(8,128)S(1)} %get-tuple-element.12.refs_3_), custom_call_target="tpu_custom_call" | custom-call | tf_op jit(solution)/shard_map/pallas_call | solution.py:132
  37.7 3.5 %collective-permute-done.13 = f32[4,24,128]{2,1,0:T(8,128)S(1)} collective-permute-done((f32[4,24,128]{2,1,0:T(8,128)S(1)}, f32[4,24,128]{2,1,0:T(8,128)S(1)}, u32[]{:S(2)}, u32[]{:S(2)}) %collective-permute-start.13) | collective-permute-done | bytes 49184 | tf_op jit(solution)/shard_map/ppermute | solution.py:211
  41.2 3.1 %collective-permute-start.14 = (f32[2,24,128]{2,1,0:T(8,128)S(1)}, f32[2,24,128]{2,1,0:T(8,128)S(1)}, u32[]{:S(2)}, u32[]{:S(2)}) collective-permute-start(f32[2,24,128]{2,1,0:T(8,128)S(1)} %get-tuple-element.23), channel_id=1, source_target_pairs={{0,40},{16,56},{4,44},{20,60},{8,32},{24,48},{12,36},{28,52},{32,8... | collective-permute-start | bytes 73736 | tf_op jit(solution)/shard_map/ppermute | solution.py:211
  44.7 2.5 %collective-permute-done.14 = f32[2,24,128]{2,1,0:T(8,128)S(1)} collective-permute-done((f32[2,24,128]{2,1,0:T(8,128)S(1)}, f32[2,24,128]{2,1,0:T(8,128)S(1)}, u32[]{:S(2)}, u32[]{:S(2)}) %collective-permute-start.14) | collective-permute-done | bytes 24608 | tf_op jit(solution)/shard_map/ppermute | solution.py:211
  47.2 1.1 %collective-permute-start.15 = (f32[1,24,128]{2,1,0:T(8,128)S(1)}, f32[1,24,128]{2,1,0:T(8,128)S(1)}, u32[]{:S(2)}, u32[]{:S(2)}) collective-permute-start(f32[1,24,128]{2,1,0:T(8,128)S(1)} %slice_add_fusion.10), channel_id=1, source_target_pairs={{0,4},{16,20},{4,0},{20,16},{8,12},{24,28},{12,8},{28,24},{32,36},... | collective-permute-start | bytes 36872 | tf_op jit(solution)/shard_map/ppermute | solution.py:232
  48.3 2.2 %collective-permute-start.9 = (f32[4,48,128]{2,1,0:T(8,128)S(1)}, f32[4,48,128]{2,1,0:T(8,128)S(1)}, u32[]{:S(2)}, u32[]{:S(2)}) collective-permute-start(f32[4,48,128]{2,1,0:T(8,128)S(1)} %get-tuple-element.17), channel_id=1, source_target_pairs={{0,3},{16,19},{4,7},{20,23},{8,11},{24,27},{12,15},{28,31},{32,35}... | collective-permute-start | bytes 294920 | tf_op jit(solution)/shard_map/ppermute | solution.py:211
  50.9 3.3 %collective-permute-done.9 = f32[4,48,128]{2,1,0:T(8,128)S(1)} collective-permute-done((f32[4,48,128]{2,1,0:T(8,128)S(1)}, f32[4,48,128]{2,1,0:T(8,128)S(1)}, u32[]{:S(2)}, u32[]{:S(2)}) %collective-permute-start.9) | collective-permute-done | bytes 98336 | tf_op jit(solution)/shard_map/ppermute | solution.py:211
  54.4 4.0 %collective-permute-done.10 = f32[2,48,128]{2,1,0:T(8,128)S(1)} collective-permute-done((f32[2,48,128]{2,1,0:T(8,128)S(1)}, f32[2,48,128]{2,1,0:T(8,128)S(1)}, u32[]{:S(2)}, u32[]{:S(2)}) %collective-permute-start.10) | collective-permute-done | bytes 49184 | tf_op jit(solution)/shard_map/ppermute | solution.py:211
  58.5 1.4 %collective-permute-start.11 = (f32[1,48,128]{2,1,0:T(8,128)S(1)}, f32[1,48,128]{2,1,0:T(8,128)S(1)}, u32[]{:S(2)}, u32[]{:S(2)}) collective-permute-start(f32[1,48,128]{2,1,0:T(8,128)S(1)} %slice_add_fusion.8), channel_id=1, source_target_pairs={{0,8},{16,24},{4,12},{20,28},{8,0},{24,16},{12,4},{28,20},{32,40},... | collective-permute-start | bytes 73736 | tf_op jit(solution)/shard_map/ppermute | solution.py:233
  60.5 2.7 %collective-permute-done.11 = f32[1,48,128]{2,1,0:T(8,128)S(1)} collective-permute-done((f32[1,48,128]{2,1,0:T(8,128)S(1)}, f32[1,48,128]{2,1,0:T(8,128)S(1)}, u32[]{:S(2)}, u32[]{:S(2)}) %collective-permute-start.11) | collective-permute-done | bytes 24608 | tf_op jit(solution)/shard_map/ppermute | solution.py:233
  (36 shorter events, 3.9 us)
Async XLA Ops:
  0.6 5.4 %collective-permute-start.4 = (f32[1,51,128]{2,1,0:T(8,128)}, f32[1,51,128]{2,1,0:T(8,128)S(1)}, u32[]{:S(2)}, u32[]{:S(2)}) collective-permute-start(f32[1,51,128]{2,1,0:T(8,128)} %bitcast.14), channel_id=1, source_target_pairs={{0,8},{16,24},{4,12},{20,28},{8,0},{24,16},{12,4},{28,20},{32,40},... | collective-permute-start | bytes 78344 | tf_op jit(solution)/shard_map/ppermute | solution.py:207
  4.0 0.7 %copy-start = (f32[51,64]{1,0:T(8,128)S(1)}, f32[51,64]{1,0:T(8,128)}, u32[]{:S(2)}) copy-start(f32[51,64]{1,0:T(8,128)} %center.1) | copy-start | bytes 39172
  4.7 1.3 %copy-start.1 = (f32[51,128]{1,0:T(8,128)S(1)}, f32[51,128]{1,0:T(8,128)}, u32[]{:S(2)}) copy-start(f32[51,128]{1,0:T(8,128)} %param.3) | copy-start | bytes 78340
  4.8 3.8 %collective-permute-start = (f32[1,26,128]{2,1,0:T(8,128)S(1)}, f32[1,26,128]{2,1,0:T(8,128)S(1)}, u32[]{:S(2)}, u32[]{:S(2)}) collective-permute-start(f32[1,26,128]{2,1,0:T(8,128)S(1)} %bitcast.10), channel_id=1, source_target_pairs={{0,4},{16,20},{4,0},{20,16},{8,12},{24,28},{12,8},{28,24},{32,36},... | collective-permute-start | bytes 39944 | tf_op jit(solution)/shard_map/ppermute | solution.py:207
  6.1 6.7 %collective-permute-start.5 = (f32[2,51,128]{2,1,0:T(8,128)S(1)}, f32[2,51,128]{2,1,0:T(8,128)S(1)}, u32[]{:S(2)}, u32[]{:S(2)}) collective-permute-start(f32[2,51,128]{2,1,0:T(8,128)S(1)} %pad_maximum_fusion.4), channel_id=1, source_target_pairs={{0,1},{16,17},{4,5},{20,21},{8,9},{24,25},{12,13},{28,29},{32,33},... | collective-permute-start | bytes 156680 | tf_op jit(solution)/shard_map/ppermute | solution.py:207
  8.6 6.4 %collective-permute-start.1 = (f32[2,26,128]{2,1,0:T(8,128)S(1)}, f32[2,26,128]{2,1,0:T(8,128)S(1)}, u32[]{:S(2)}, u32[]{:S(2)}) collective-permute-start(f32[2,26,128]{2,1,0:T(8,128)S(1)} %pad_maximum_fusion.5), channel_id=1, source_target_pairs={{0,40},{16,56},{4,44},{20,60},{8,32},{24,48},{12,36},{28,52},{32,8... | collective-permute-start | bytes 79880 | tf_op jit(solution)/shard_map/ppermute | solution.py:207
  12.8 6.1 %collective-permute-start.6 = (f32[4,51,128]{2,1,0:T(8,128)S(1)}, f32[4,51,128]{2,1,0:T(8,128)S(1)}, u32[]{:S(2)}, u32[]{:S(2)}) collective-permute-start(f32[4,51,128]{2,1,0:T(8,128)S(1)} %pad_maximum_fusion.2), channel_id=1, source_target_pairs={{0,3},{16,19},{4,7},{20,23},{8,11},{24,27},{12,15},{28,31},{32,35}... | collective-permute-start | bytes 313352 | tf_op jit(solution)/shard_map/ppermute | solution.py:207
  15.0 4.4 %collective-permute-start.2 = (f32[4,26,128]{2,1,0:T(8,128)S(1)}, f32[4,26,128]{2,1,0:T(8,128)S(1)}, u32[]{:S(2)}, u32[]{:S(2)}) collective-permute-start(f32[4,26,128]{2,1,0:T(8,128)S(1)} %pad_maximum_fusion.3), channel_id=1, source_target_pairs={{0,64},{16,80},{4,68},{20,84},{8,72},{24,88},{12,76},{28,92},{32,9... | collective-permute-start | bytes 159752 | tf_op jit(solution)/shard_map/ppermute | solution.py:207
  18.9 7.4 %collective-permute-start.7 = (f32[8,51,128]{2,1,0:T(8,128)S(1)}, f32[8,51,128]{2,1,0:T(8,128)S(1)}, u32[]{:S(2)}, u32[]{:S(2)}) collective-permute-start(f32[8,51,128]{2,1,0:T(8,128)S(1)} %pad_maximum_fusion.refs_1_), channel_id=1, source_target_pairs={{0,16},{16,0},{4,20},{20,4},{8,24},{24,8},{12,28},{28,12},{32,48},... | collective-permute-start | bytes 626696 | tf_op jit(solution)/shard_map/ppermute | solution.py:207
  19.4 6.9 %collective-permute-start.3 = (f32[8,26,128]{2,1,0:T(8,128)S(1)}, f32[8,26,128]{2,1,0:T(8,128)S(1)}, u32[]{:S(2)}, u32[]{:S(2)}) collective-permute-start(f32[8,26,128]{2,1,0:T(8,128)S(1)} %pad_maximum_fusion.1.refs_0_), channel_id=1, source_target_pairs={{0,192},{16,208},{4,196},{20,212},{8,200},{24,216},{12,204},{28,22... | collective-permute-start | bytes 319496 | tf_op jit(solution)/shard_map/ppermute | solution.py:207
  30.9 6.1 %collective-permute-start.12 = (f32[8,24,128]{2,1,0:T(8,128)S(1)}, f32[8,24,128]{2,1,0:T(8,128)S(1)}, u32[]{:S(2)}, u32[]{:S(2)}) collective-permute-start(f32[8,24,128]{2,1,0:T(8,128)S(1)} %get-tuple-element.15), channel_id=1, source_target_pairs={{0,192},{16,208},{4,196},{20,212},{8,200},{24,216},{12,204},{28,22... | collective-permute-start | bytes 294920 | tf_op jit(solution)/shard_map/ppermute | solution.py:211
  37.0 0.7 %copy-start.2 = (f32[48,4]{0,1:T(4,128)S(1)}, f32[48,4]{0,1:T(4,128)}, u32[]{:S(2)}) copy-start(f32[48,4]{0,1:T(4,128)} %param.5) | copy-start | bytes 2308
  37.0 4.2 %collective-permute-start.13 = (f32[4,24,128]{2,1,0:T(8,128)S(1)}, f32[4,24,128]{2,1,0:T(8,128)S(1)}, u32[]{:S(2)}, u32[]{:S(2)}) collective-permute-start(f32[4,24,128]{2,1,0:T(8,128)S(1)} %get-tuple-element.19), channel_id=1, source_target_pairs={{0,64},{16,80},{4,68},{20,84},{8,72},{24,88},{12,76},{28,92},{32,9... | collective-permute-start | bytes 147464 | tf_op jit(solution)/shard_map/ppermute | solution.py:211
  41.2 6.0 %collective-permute-start.14 = (f32[2,24,128]{2,1,0:T(8,128)S(1)}, f32[2,24,128]{2,1,0:T(8,128)S(1)}, u32[]{:S(2)}, u32[]{:S(2)}) collective-permute-start(f32[2,24,128]{2,1,0:T(8,128)S(1)} %get-tuple-element.23), channel_id=1, source_target_pairs={{0,40},{16,56},{4,44},{20,60},{8,32},{24,48},{12,36},{28,52},{32,8... | collective-permute-start | bytes 73736 | tf_op jit(solution)/shard_map/ppermute | solution.py:211
  44.6 3.7 %collective-permute-start.8 = (f32[8,48,128]{2,1,0:T(8,128)S(1)}, f32[8,48,128]{2,1,0:T(8,128)S(1)}, u32[]{:S(2)}, u32[]{:S(2)}) collective-permute-start(f32[8,48,128]{2,1,0:T(8,128)S(1)} %get-tuple-element.13), channel_id=1, source_target_pairs={{0,16},{16,0},{4,20},{20,4},{8,24},{24,8},{12,28},{28,12},{32,48},... | collective-permute-start | bytes 589832 | tf_op jit(solution)/shard_map/ppermute | solution.py:211
  47.2 3.7 %collective-permute-start.15 = (f32[1,24,128]{2,1,0:T(8,128)S(1)}, f32[1,24,128]{2,1,0:T(8,128)S(1)}, u32[]{:S(2)}, u32[]{:S(2)}) collective-permute-start(f32[1,24,128]{2,1,0:T(8,128)S(1)} %slice_add_fusion.10), channel_id=1, source_target_pairs={{0,4},{16,20},{4,0},{20,16},{8,12},{24,28},{12,8},{28,24},{32,36},... | collective-permute-start | bytes 36872 | tf_op jit(solution)/shard_map/ppermute | solution.py:232
  48.3 5.9 %collective-permute-start.9 = (f32[4,48,128]{2,1,0:T(8,128)S(1)}, f32[4,48,128]{2,1,0:T(8,128)S(1)}, u32[]{:S(2)}, u32[]{:S(2)}) collective-permute-start(f32[4,48,128]{2,1,0:T(8,128)S(1)} %get-tuple-element.17), channel_id=1, source_target_pairs={{0,3},{16,19},{4,7},{20,23},{8,11},{24,27},{12,15},{28,31},{32,35}... | collective-permute-start | bytes 294920 | tf_op jit(solution)/shard_map/ppermute | solution.py:211
  54.3 4.2 %collective-permute-start.10 = (f32[2,48,128]{2,1,0:T(8,128)S(1)}, f32[2,48,128]{2,1,0:T(8,128)S(1)}, u32[]{:S(2)}, u32[]{:S(2)}) collective-permute-start(f32[2,48,128]{2,1,0:T(8,128)S(1)} %get-tuple-element.21), channel_id=1, source_target_pairs={{0,1},{16,17},{4,5},{20,21},{8,9},{24,25},{12,13},{28,29},{32,33},... | collective-permute-start | bytes 147464 | tf_op jit(solution)/shard_map/ppermute | solution.py:211
  58.5 4.7 %collective-permute-start.11 = (f32[1,48,128]{2,1,0:T(8,128)S(1)}, f32[1,48,128]{2,1,0:T(8,128)S(1)}, u32[]{:S(2)}, u32[]{:S(2)}) collective-permute-start(f32[1,48,128]{2,1,0:T(8,128)S(1)} %slice_add_fusion.8), channel_id=1, source_target_pairs={{0,8},{16,24},{4,12},{20,28},{8,0},{24,16},{12,4},{28,20},{32,40},... | collective-permute-start | bytes 73736 | tf_op jit(solution)/shard_map/ppermute | solution.py:233
where the time goes:
time: 64.8 us; the launch traced here: 63.8 us
  starting transfers between devices  27.6 us (43%)
  waiting for transfers between devices  22.7 us (35%)
  Pallas kernels  9.79 us (15%)
  local copies, waits for them, and re-layouts  1.39 us (2%)
  other arithmetic  1.35 us (2%)
  between operations  0.72 us (1%)
    ppermute x8, starting transfers between devices, gather_step(): return (held, lax.ppermute(held, AXES, stage))  16.3 us
    ppermute x6, waiting for transfers between devices, sum_step(): arrived = lax.ppermute(theirs, AXES, stage)  13.7 us
    pallas_call x3, Pallas kernels, quad(): pl.pallas_call(body, out_shape=(jax.ShapeDtypeStruct((hc, COLS // 2, LANE...  9.72 us
    ppermute x6, starting transfers between devices, sum_step(): arrived = lax.ppermute(theirs, AXES, stage)  8.82 us
    ppermute x8, waiting for transfers between devices, gather_step(): return (held, lax.ppermute(held, AXES, stage))  5.89 us
    ppermute x1, waiting for transfers between devices, per_device(): motion = (motion + lax.ppermute(motion_away, AXES, FLUID_STAGES[0]))[0]  2.73 us
    ppermute x1, starting transfers between devices, per_device(): motion = (motion + lax.ppermute(motion_away, AXES, FLUID_STAGES[0]))[0]  1.39 us
    unnamed x6, local copies, waits for them, and re-layouts  1.32 us
  transfers between devices with their start and end apart: 16, of which 12 were waited for; matrix products, arithmetic and copies ran while one was open for 2% of the time, Pallas kernels for 8%

commit v1 on v0

--- a/solution.py
+++ b/solution.py
@@ -45,7 +45,7 @@
     cpos, cval, fval, fpos, t0, t1, acc, loads = refs[n + 1 + nfl:]
     hf = fluids[0].shape[0]
     nf = nfl * hf
-    nb = center.shape[0] // 2
+    nb = center.shape[0] // 52
     half = lax.broadcasted_iota(jnp.int32, (1, LANES), 1) < LANES // 2
     for k in range(nf):
         s = slice(k * LANES, (k + 1) * LANES)
@@ -56,16 +56,20 @@
         fval[COLS:2 * COLS, s] = val - hi
         fpos[:, s] = chunk[0:3, :] * float(WAVES)
     for b in range(nb):
-        one = center[2 * b]
-        two = center[2 * b + 1]
+        one = center[48 * b:48 * b + 24, :]
+        two = center[48 * b + 24:48 * b + 48, :]
         top = jnp.where(half, one, pltpu.roll(two, LANES // 2, 1))
         bot = jnp.where(half, pltpu.roll(one, LANES // 2, 1), two)
-        val = jnp.concatenate([top[0:24], bot[0:24]], 0) * LEAD
+        val = jnp.concatenate([top, bot], 0) * LEAD
         hi = high(val)
         v = jnp.concatenate([hi, val - hi], 0)
         cval[b, :, 0:LANES] = v
         cval[b, :, LANES:2 * LANES] = v
-        pos = jnp.concatenate([top[24:26], bot[24:25], jnp.zeros((5, LANES), jnp.float32)], 0) * float(WAVES)
+        place_one = center[48 * nb + 4 * b:48 * nb + 4 * b + 2, :]
+        place_two = center[48 * nb + 4 * b + 2:48 * nb + 4 * b + 4, :]
+        top = jnp.where(half, place_one, pltpu.roll(place_two, LANES // 2, 1))
+        bot = jnp.where(half, pltpu.roll(place_one, LANES // 2, 1), place_two)
+        pos = jnp.concatenate([top, bot[0:1], jnp.zeros((5, LANES), jnp.float32)], 0) * float(WAVES)
         post = jnp.transpose(pos)
         for a in range(3):
             cpos[a, b * LANES:(b + 1) * LANES, :] = jnp.broadcast_to(post[:, a:a + 1], (LANES, LANES))
@@ -120,8 +124,8 @@
 
 def quad(center, fluids, load=None, motion=None):
     hf = fluids[0].shape[0]
-    hc = center.shape[0]
-    nb = hc // 2
+    nb = center.shape[0] // 52
+    hc = 2 * nb
     width = len(fluids) * hf * LANES
     extra = tuple(a for a in (load, motion) if a is not None)
 
@@ -189,22 +193,35 @@
     return 3 - v
 
 
+def first_hop(v, core):
+    return wrap(v) if core else near(v)
+
+
+def second_hop(v, core):
+    return near(v) if core else wrap(v)
+
+
 FLUID_STAGES = (
     partners(lambda x, y, z, c: (x, y, z ^ 2, c)),
-    partners(lambda x, y, z, c: (near(x), y, z, c)),
-    partners(lambda x, y, z, c: (wrap(x), y, z, c)),
+    partners(lambda x, y, z, c: (first_hop(x, c), y, z, c)),
+    partners(lambda x, y, z, c: (second_hop(x, c), y, z, c)),
     partners(lambda x, y, z, c: (x, y, z, 1 - c)),
 )
 CENTER_STAGES = (
-    partners(lambda x, y, z, c: (x, y, z ^ 1, c)),
-    partners(lambda x, y, z, c: (x, y, 2 * wrap(z // 2) + z % 2, c)),
-    partners(lambda x, y, z, c: (x, near(y), z, c)),
-    partners(lambda x, y, z, c: (x, wrap(y), z, c)),
+    partners(lambda x, y, z, c: (x, y, 2 * wrap(z // 2) + z % 2 if c else z ^ 1, c)),
+    partners(lambda x, y, z, c: (x, y, z ^ 1 if c else 2 * wrap(z // 2) + z % 2, c)),
+    partners(lambda x, y, z, c: (x, first_hop(y, c), z, c)),
+    partners(lambda x, y, z, c: (x, second_hop(y, c), z, c)),
 )
 
 
 def gather_step(held, stage):
     return held, lax.ppermute(held, AXES, stage)
+
+
+def center_rows(mine, theirs):
+    cut = mine.shape[0] // 26 * 24
+    return jnp.concatenate([mine[:cut], theirs[:cut], mine[cut:], theirs[cut:]], 0)
 
 
 def sum_step(mine, theirs, stage):
@@ -215,11 +232,11 @@
 
 def per_device(fluid_data, center_data, poly_coef):
     fluid = fluid_data[None]
-    center = packed(center_data)[None]
+    center = packed(center_data)
     fluids = (fluid, None)
     centers = (center, None)
     for i in range(4):
-        held = centers[0] if i == 0 else jnp.concatenate(centers, 0)
+        held = centers[0] if i == 0 else center_rows(*centers)
         centers = gather_step(held, CENTER_STAGES[i])
         held = fluids[0] if i == 0 else jnp.concatenate(fluids, 0)
         fluids = gather_step(held, FLUID_STAGES[i])

time: 64.8 us -> 74.7 us (1.15)
  the two profiles are of different devices: /device:TPU:32 before, /device:TPU:24 now
where the time goes in v1:
time: 74.7 us; the launch traced here: 74.5 us
  waiting for transfers between devices  33.2 us (44%)
  starting transfers between devices  27.7 us (37%)
  Pallas kernels  9.82 us (13%)
  other arithmetic  2.1 us (3%)
    ppermute x8, starting transfers between devices, gather_step(): return (held, lax.ppermute(held, AXES, stage))  17 us
    ppermute x6, waiting for transfers between devices, sum_step(): arrived = lax.ppermute(theirs, AXES, stage)  15.8 us
    ppermute x8, waiting for transfers between devices, gather_step(): return (held, lax.ppermute(held, AXES, stage))  15.1 us
    pallas_call x3, Pallas kernels, quad(): pl.pallas_call(body, out_shape=(jax.ShapeDtypeStruct((hc, COLS // 2, LANE...  9.74 us
    ppermute x6, starting transfers between devices, sum_step(): arrived = lax.ppermute(theirs, AXES, stage)  7.31 us
    ppermute x1, waiting for transfers between devices, per_device(): motion = (motion + lax.ppermute(motion_away, AXES, FLUID_STAGES[0]))[0]  2.33 us
    ppermute x1, starting transfers between devices, per_device(): motion = (motion + lax.ppermute(motion_away, AXES, FLUID_STAGES[0]))[0]  1.93 us
  transfers between devices with their start and end apart: 16, of which 12 were waited for; matrix products, arithmetic and copies ran while one was open for 1% of the time, Pallas kernels for 7%

profile of v1, /device:TPU:24, one launch (start us, length us, event | category | flops | bytes accessed | tf_op | source)
XLA Modules:
  0.0 74.5 jit_solution(6444148794423023392)
XLA Ops:
  0.6 3.4 %collective-permute-start.4 = (f32[1,51,128]{2,1,0:T(8,128)}, f32[1,51,128]{2,1,0:T(8,128)S(1)}, u32[]{:S(2)}, u32[]{:S(2)}) collective-permute-start(f32[1,51,128]{2,1,0:T(8,128)} %bitcast.9), channel_id=1, source_target_pairs={{0,8},{16,24},{4,12},{20,28},{8,0},{24,16},{12,4},{28,20},{32,40},... | collective-permute-start | bytes 78344 | tf_op jit(solution)/shard_map/ppermute | solution.py:219
  4.0 2.1 %collective-permute-done.4 = f32[1,51,128]{2,1,0:T(8,128)S(1)} collective-permute-done((f32[1,51,128]{2,1,0:T(8,128)}, f32[1,51,128]{2,1,0:T(8,128)S(1)}, u32[]{:S(2)}, u32[]{:S(2)}) %collective-permute-start.4) | collective-permute-done | bytes 26144 | tf_op jit(solution)/shard_map/ppermute | solution.py:219
  6.8 1.5 %collective-permute-start.5 = (f32[2,51,128]{2,1,0:T(8,128)S(1)}, f32[2,51,128]{2,1,0:T(8,128)S(1)}, u32[]{:S(2)}, u32[]{:S(2)}) collective-permute-start(f32[2,51,128]{2,1,0:T(8,128)S(1)} %pad_maximum_fusion.2), channel_id=1, source_target_pairs={{0,1},{16,19},{4,5},{20,23},{8,9},{24,27},{12,13},{28,31},{32,33},... | collective-permute-start | bytes 156680 | tf_op jit(solution)/shard_map/ppermute | solution.py:219
  8.3 2.7 %collective-permute-done.5 = f32[2,51,128]{2,1,0:T(8,128)S(1)} collective-permute-done((f32[2,51,128]{2,1,0:T(8,128)S(1)}, f32[2,51,128]{2,1,0:T(8,128)S(1)}, u32[]{:S(2)}, u32[]{:S(2)}) %collective-permute-start.5) | collective-permute-done | bytes 52256 | tf_op jit(solution)/shard_map/ppermute | solution.py:219
  11.0 2.8 %collective-permute-start.6 = (f32[4,51,128]{2,1,0:T(8,128)S(1)}, f32[4,51,128]{2,1,0:T(8,128)S(1)}, u32[]{:S(2)}, u32[]{:S(2)}) collective-permute-start(f32[4,51,128]{2,1,0:T(8,128)S(1)} %pad_maximum_fusion.1), channel_id=1, source_target_pairs={{0,3},{16,17},{4,7},{20,21},{8,11},{24,25},{12,15},{28,29},{32,35}... | collective-permute-start | bytes 313352 | tf_op jit(solution)/shard_map/ppermute | solution.py:219
  13.9 1.9 %collective-permute-start = (f32[26,128]{1,0:T(8,128)S(1)}, f32[26,128]{1,0:T(8,128)S(1)}, u32[]{:S(2)}, u32[]{:S(2)}) collective-permute-start(f32[26,128]{1,0:T(8,128)S(1)} %pack.1), channel_id=1, source_target_pairs={{0,4},{16,56},{4,0},{20,60},{8,12},{24,48},{12,8},{28,52},{32,36},... | collective-permute-start | bytes 39944 | tf_op jit(solution)/shard_map/ppermute | solution.py:219
  15.9 2.0 %collective-permute-done = f32[26,128]{1,0:T(8,128)S(1)} collective-permute-done((f32[26,128]{1,0:T(8,128)S(1)}, f32[26,128]{1,0:T(8,128)S(1)}, u32[]{:S(2)}, u32[]{:S(2)}) %collective-permute-start) | collective-permute-done | bytes 13344 | tf_op jit(solution)/shard_map/ppermute | solution.py:219
  18.0 5.9 %collective-permute-start.1 = (f32[52,128]{1,0:T(8,128)S(1)}, f32[52,128]{1,0:T(8,128)S(1)}, u32[]{:S(2)}, u32[]{:S(2)}) collective-permute-start(f32[52,128]{1,0:T(8,128)S(1)} %pad_maximum_fusion.3), channel_id=1, source_target_pairs={{0,40},{16,20},{4,44},{20,16},{8,32},{24,28},{12,36},{28,24},{32,8... | collective-permute-start | bytes 79880 | tf_op jit(solution)/shard_map/ppermute | solution.py:219
  23.9 1.9 %collective-permute-done.1 = f32[52,128]{1,0:T(8,128)S(1)} collective-permute-done((f32[52,128]{1,0:T(8,128)S(1)}, f32[52,128]{1,0:T(8,128)S(1)}, u32[]{:S(2)}, u32[]{:S(2)}) %collective-permute-start.1) | collective-permute-done | bytes 26656 | tf_op jit(solution)/shard_map/ppermute | solution.py:219
  26.6 3.7 %collective-permute-done.2 = f32[104,128]{1,0:T(8,128)S(1)} collective-permute-done((f32[104,128]{1,0:T(8,128)S(1)}, f32[104,128]{1,0:T(8,128)S(1)}, u32[]{:S(2)}, u32[]{:S(2)}) %collective-permute-start.2) | collective-permute-done | bytes 53280 | tf_op jit(solution)/shard_map/ppermute | solution.py:219
  30.9 2.5 %shard_map.50 = (f32[8,24,128]{2,1,0:T(8,128)S(1)}, f32[8,48,128]{2,1,0:T(8,128)S(1)}) custom-call(f32[208,128]{1,0:T(8,128)S(1)} %concatenate.33.refs_0_, f32[8,51,128]{2,1,0:T(8,128)S(1)} %pad_maximum_fusion.refs_1_), custom_call_target="tpu_custom_call" | custom-call | tf_op jit(solution)/shard_map/pallas_call | solution.py:136
  33.4 2.9 %collective-permute-done.3.refs_0_ = f32[208,128]{1,0:T(8,128)S(1)} collective-permute-done((f32[208,128]{1,0:T(8,128)S(1)}, f32[208,128]{1,0:T(8,128)S(1)}, u32[]{:S(2)}, u32[]{:S(2)}) %collective-permute-start.3) | collective-permute-done | bytes 106528 | tf_op jit(solution)/shard_map/ppermute | solution.py:219
  36.3 4.6 %shard_map.51 = (f32[8,24,128]{2,1,0:T(8,128)S(1)}, f32[8,48,128]{2,1,0:T(8,128)S(1)}, f32[8,48,128]{2,1,0:T(8,128)S(1)}) custom-call(f32[208,128]{1,0:T(8,128)S(1)} %collective-permute-done.3.refs_0_, f32[8,51,128]{2,1,0:T(8,128)S(1)} %pad_maximum_fusion.refs_1_, f32[8,51,128]{2,1,0:T(8,128)S(1)} %collective-permute-done.7.refs_2_.refs_1_, ...), custom_call_target="tpu_custom_call" | custom-call | tf_op jit(solution)/shard_map/pallas_call | solution.py:136
  41.7 2.6 %shard_map.52 = (f32[8,24,128]{2,1,0:T(8,128)S(1)}, f32[8,48,128]{2,1,0:T(8,128)S(1)}) custom-call(f32[208,128]{1,0:T(8,128)S(1)} %concatenate.33.refs_0_, f32[8,51,128]{2,1,0:T(8,128)S(1)} %collective-permute-done.7.refs_2_.refs_1_, f32[8,24,128]{2,1,0:T(8,128)S(1)} %get-tuple-element.11.refs_2_, f32[8,48,128]{2,1,0:T(8,128)S(1)} %get-tuple-element.12.refs_3_), custom_call_target="tpu_custom_call" | custom-call | tf_op jit(solution)/shard_map/pallas_call | solution.py:136
  44.3 2.7 %collective-permute-done.12 = f32[8,24,128]{2,1,0:T(8,128)S(1)} collective-permute-done((f32[8,24,128]{2,1,0:T(8,128)S(1)}, f32[8,24,128]{2,1,0:T(8,128)S(1)}, u32[]{:S(2)}, u32[]{:S(2)}) %collective-permute-start.12) | collective-permute-done | bytes 98336 | tf_op jit(solution)/shard_map/ppermute | solution.py:228
  47.7 3.5 %collective-permute-done.13 = f32[4,24,128]{2,1,0:T(8,128)S(1)} collective-permute-done((f32[4,24,128]{2,1,0:T(8,128)S(1)}, f32[4,24,128]{2,1,0:T(8,128)S(1)}, u32[]{:S(2)}, u32[]{:S(2)}) %collective-permute-start.13) | collective-permute-done | bytes 49184 | tf_op jit(solution)/shard_map/ppermute | solution.py:228
  51.2 4.0 %collective-permute-start.14 = (f32[2,24,128]{2,1,0:T(8,128)S(1)}, f32[2,24,128]{2,1,0:T(8,128)S(1)}, u32[]{:S(2)}, u32[]{:S(2)}) collective-permute-start(f32[2,24,128]{2,1,0:T(8,128)S(1)} %get-tuple-element.23), channel_id=1, source_target_pairs={{0,40},{16,20},{4,44},{20,16},{8,32},{24,28},{12,36},{28,24},{32,8... | collective-permute-start | bytes 73736 | tf_op jit(solution)/shard_map/ppermute | solution.py:228
  55.6 1.8 %collective-permute-done.14 = f32[2,24,128]{2,1,0:T(8,128)S(1)} collective-permute-done((f32[2,24,128]{2,1,0:T(8,128)S(1)}, f32[2,24,128]{2,1,0:T(8,128)S(1)}, u32[]{:S(2)}, u32[]{:S(2)}) %collective-permute-start.14) | collective-permute-done | bytes 24608 | tf_op jit(solution)/shard_map/ppermute | solution.py:228
  57.3 1.5 %collective-permute-start.15 = (f32[1,24,128]{2,1,0:T(8,128)S(1)}, f32[1,24,128]{2,1,0:T(8,128)S(1)}, u32[]{:S(2)}, u32[]{:S(2)}) collective-permute-start(f32[1,24,128]{2,1,0:T(8,128)S(1)} %slice_add_fusion.10), channel_id=1, source_target_pairs={{0,4},{16,56},{4,0},{20,60},{8,12},{24,48},{12,8},{28,52},{32,36},... | collective-permute-start | bytes 36872 | tf_op jit(solution)/shard_map/ppermute | solution.py:249
  58.8 2.2 %collective-permute-start.9 = (f32[4,48,128]{2,1,0:T(8,128)S(1)}, f32[4,48,128]{2,1,0:T(8,128)S(1)}, u32[]{:S(2)}, u32[]{:S(2)}) collective-permute-start(f32[4,48,128]{2,1,0:T(8,128)S(1)} %get-tuple-element.17), channel_id=1, source_target_pairs={{0,3},{16,17},{4,7},{20,21},{8,11},{24,25},{12,15},{28,29},{32,35}... | collective-permute-start | bytes 294920 | tf_op jit(solution)/shard_map/ppermute | solution.py:228
  61.1 3.8 %collective-permute-done.9 = f32[4,48,128]{2,1,0:T(8,128)S(1)} collective-permute-done((f32[4,48,128]{2,1,0:T(8,128)S(1)}, f32[4,48,128]{2,1,0:T(8,128)S(1)}, u32[]{:S(2)}, u32[]{:S(2)}) %collective-permute-start.9) | collective-permute-done | bytes 98336 | tf_op jit(solution)/shard_map/ppermute | solution.py:228
  65.1 4.0 %collective-permute-done.10 = f32[2,48,128]{2,1,0:T(8,128)S(1)} collective-permute-done((f32[2,48,128]{2,1,0:T(8,128)S(1)}, f32[2,48,128]{2,1,0:T(8,128)S(1)}, u32[]{:S(2)}, u32[]{:S(2)}) %collective-permute-start.10) | collective-permute-done | bytes 49184 | tf_op jit(solution)/shard_map/ppermute | solution.py:228
  69.1 1.9 %collective-permute-start.11 = (f32[1,48,128]{2,1,0:T(8,128)S(1)}, f32[1,48,128]{2,1,0:T(8,128)S(1)}, u32[]{:S(2)}, u32[]{:S(2)}) collective-permute-start(f32[1,48,128]{2,1,0:T(8,128)S(1)} %slice_add_fusion.8), channel_id=1, source_target_pairs={{0,8},{16,24},{4,12},{20,28},{8,0},{24,16},{12,4},{28,20},{32,40},... | collective-permute-start | bytes 73736 | tf_op jit(solution)/shard_map/ppermute | solution.py:250
  71.6 2.3 %collective-permute-done.11 = f32[1,48,128]{2,1,0:T(8,128)S(1)} collective-permute-done((f32[1,48,128]{2,1,0:T(8,128)S(1)}, f32[1,48,128]{2,1,0:T(8,128)S(1)}, u32[]{:S(2)}, u32[]{:S(2)}) %collective-permute-start.11) | collective-permute-done | bytes 24608 | tf_op jit(solution)/shard_map/ppermute | solution.py:250
  (44 shorter events, 5.7 us)
Async XLA Ops:
  0.6 10.4 %copy-start.1 = (f32[51,128]{1,0:T(8,128)S(1)}, f32[51,128]{1,0:T(8,128)}, u32[]{:S(2)}) copy-start(f32[51,128]{1,0:T(8,128)} %param.3) | copy-start | bytes 78340
  0.6 5.4 %collective-permute-start.4 = (f32[1,51,128]{2,1,0:T(8,128)}, f32[1,51,128]{2,1,0:T(8,128)S(1)}, u32[]{:S(2)}, u32[]{:S(2)}) collective-permute-start(f32[1,51,128]{2,1,0:T(8,128)} %bitcast.9), channel_id=1, source_target_pairs={{0,8},{16,24},{4,12},{20,28},{8,0},{24,16},{12,4},{28,20},{32,40},... | collective-permute-start | bytes 78344 | tf_op jit(solution)/shard_map/ppermute | solution.py:219
  6.8 7.0 %copy-start = (f32[51,64]{1,0:T(8,128)S(1)}, f32[51,64]{1,0:T(8,128)}, u32[]{:S(2)}) copy-start(f32[51,64]{1,0:T(8,128)} %center.1) | copy-start | bytes 39172
  6.8 4.2 %collective-permute-start.5 = (f32[2,51,128]{2,1,0:T(8,128)S(1)}, f32[2,51,128]{2,1,0:T(8,128)S(1)}, u32[]{:S(2)}, u32[]{:S(2)}) collective-permute-start(f32[2,51,128]{2,1,0:T(8,128)S(1)} %pad_maximum_fusion.2), channel_id=1, source_target_pairs={{0,1},{16,19},{4,5},{20,23},{8,9},{24,27},{12,13},{28,31},{32,33},... | collective-permute-start | bytes 156680 | tf_op jit(solution)/shard_map/ppermute | solution.py:219
  11.0 6.9 %collective-permute-start.6 = (f32[4,51,128]{2,1,0:T(8,128)S(1)}, f32[4,51,128]{2,1,0:T(8,128)S(1)}, u32[]{:S(2)}, u32[]{:S(2)}) collective-permute-start(f32[4,51,128]{2,1,0:T(8,128)S(1)} %pad_maximum_fusion.1), channel_id=1, source_target_pairs={{0,3},{16,17},{4,7},{20,21},{8,11},{24,25},{12,15},{28,29},{32,35}... | collective-permute-start | bytes 313352 | tf_op jit(solution)/shard_map/ppermute | solution.py:219
  13.9 3.9 %collective-permute-start = (f32[26,128]{1,0:T(8,128)S(1)}, f32[26,128]{1,0:T(8,128)S(1)}, u32[]{:S(2)}, u32[]{:S(2)}) collective-permute-start(f32[26,128]{1,0:T(8,128)S(1)} %pack.1), channel_id=1, source_target_pairs={{0,4},{16,56},{4,0},{20,60},{8,12},{24,48},{12,8},{28,52},{32,36},... | collective-permute-start | bytes 39944 | tf_op jit(solution)/shard_map/ppermute | solution.py:219
  17.9 18.4 %collective-permute-start.7 = (f32[8,51,128]{2,1,0:T(8,128)S(1)}, f32[8,51,128]{2,1,0:T(8,128)S(1)}, u32[]{:S(2)}, u32[]{:S(2)}) collective-permute-start(f32[8,51,128]{2,1,0:T(8,128)S(1)} %pad_maximum_fusion.refs_1_), channel_id=1, source_target_pairs={{0,16},{16,0},{4,20},{20,4},{8,24},{24,8},{12,28},{28,12},{32,48},... | collective-permute-start | bytes 626696 | tf_op jit(solution)/shard_map/ppermute | solution.py:219
  18.0 7.7 %collective-permute-start.1 = (f32[52,128]{1,0:T(8,128)S(1)}, f32[52,128]{1,0:T(8,128)S(1)}, u32[]{:S(2)}, u32[]{:S(2)}) collective-permute-start(f32[52,128]{1,0:T(8,128)S(1)} %pad_maximum_fusion.3), channel_id=1, source_target_pairs={{0,40},{16,20},{4,44},{20,16},{8,32},{24,28},{12,36},{28,24},{32,8... | collective-permute-start | bytes 79880 | tf_op jit(solution)/shard_map/ppermute | solution.py:219
  25.8 4.5 %collective-permute-start.2 = (f32[104,128]{1,0:T(8,128)S(1)}, f32[104,128]{1,0:T(8,128)S(1)}, u32[]{:S(2)}, u32[]{:S(2)}) collective-permute-start(f32[104,128]{1,0:T(8,128)S(1)} %concatenate.32), channel_id=1, source_target_pairs={{0,64},{16,208},{4,68},{20,212},{8,72},{24,216},{12,76},{28,220},{... | collective-permute-start | bytes 159752 | tf_op jit(solution)/shard_map/ppermute | solution.py:219
  30.3 6.0 %collective-permute-start.3 = (f32[208,128]{1,0:T(8,128)S(1)}, f32[208,128]{1,0:T(8,128)S(1)}, u32[]{:S(2)}, u32[]{:S(2)}) collective-permute-start(f32[208,128]{1,0:T(8,128)S(1)} %concatenate.33.refs_0_), channel_id=1, source_target_pairs={{0,192},{16,80},{4,196},{20,84},{8,200},{24,88},{12,204},{28,92},{... | collective-permute-start | bytes 319496 | tf_op jit(solution)/shard_map/ppermute | solution.py:219
  40.9 6.1 %collective-permute-start.12 = (f32[8,24,128]{2,1,0:T(8,128)S(1)}, f32[8,24,128]{2,1,0:T(8,128)S(1)}, u32[]{:S(2)}, u32[]{:S(2)}) collective-permute-start(f32[8,24,128]{2,1,0:T(8,128)S(1)} %get-tuple-element.15), channel_id=1, source_target_pairs={{0,192},{16,80},{4,196},{20,84},{8,200},{24,88},{12,204},{28,92},{... | collective-permute-start | bytes 294920 | tf_op jit(solution)/shard_map/ppermute | solution.py:228
  47.0 0.7 copy-start.2
  47.0 4.2 %collective-permute-start.13 = (f32[4,24,128]{2,1,0:T(8,128)S(1)}, f32[4,24,128]{2,1,0:T(8,128)S(1)}, u32[]{:S(2)}, u32[]{:S(2)}) collective-permute-start(f32[4,24,128]{2,1,0:T(8,128)S(1)} %get-tuple-element.19), channel_id=1, source_target_pairs={{0,64},{16,208},{4,68},{20,212},{8,72},{24,216},{12,76},{28,220},{... | collective-permute-start | bytes 147464 | tf_op jit(solution)/shard_map/ppermute | solution.py:228
  51.2 6.1 %collective-permute-start.14 = (f32[2,24,128]{2,1,0:T(8,128)S(1)}, f32[2,24,128]{2,1,0:T(8,128)S(1)}, u32[]{:S(2)}, u32[]{:S(2)}) collective-permute-start(f32[2,24,128]{2,1,0:T(8,128)S(1)} %get-tuple-element.23), channel_id=1, source_target_pairs={{0,40},{16,20},{4,44},{20,16},{8,32},{24,28},{12,36},{28,24},{32,8... | collective-permute-start | bytes 73736 | tf_op jit(solution)/shard_map/ppermute | solution.py:228
  55.5 3.3 %collective-permute-start.8 = (f32[8,48,128]{2,1,0:T(8,128)S(1)}, f32[8,48,128]{2,1,0:T(8,128)S(1)}, u32[]{:S(2)}, u32[]{:S(2)}) collective-permute-start(f32[8,48,128]{2,1,0:T(8,128)S(1)} %get-tuple-element.13), channel_id=1, source_target_pairs={{0,16},{16,0},{4,20},{20,4},{8,24},{24,8},{12,28},{28,12},{32,48},... | collective-permute-start | bytes 589832 | tf_op jit(solution)/shard_map/ppermute | solution.py:228
  57.3 3.7 %collective-permute-start.15 = (f32[1,24,128]{2,1,0:T(8,128)S(1)}, f32[1,24,128]{2,1,0:T(8,128)S(1)}, u32[]{:S(2)}, u32[]{:S(2)}) collective-permute-start(f32[1,24,128]{2,1,0:T(8,128)S(1)} %slice_add_fusion.10), channel_id=1, source_target_pairs={{0,4},{16,56},{4,0},{20,60},{8,12},{24,48},{12,8},{28,52},{32,36},... | collective-permute-start | bytes 36872 | tf_op jit(solution)/shard_map/ppermute | solution.py:249
  58.8 6.0 %collective-permute-start.9 = (f32[4,48,128]{2,1,0:T(8,128)S(1)}, f32[4,48,128]{2,1,0:T(8,128)S(1)}, u32[]{:S(2)}, u32[]{:S(2)}) collective-permute-start(f32[4,48,128]{2,1,0:T(8,128)S(1)} %get-tuple-element.17), channel_id=1, source_target_pairs={{0,3},{16,17},{4,7},{20,21},{8,11},{24,25},{12,15},{28,29},{32,35}... | collective-permute-start | bytes 294920 | tf_op jit(solution)/shard_map/ppermute | solution.py:228
  64.9 4.2 %collective-permute-start.10 = (f32[2,48,128]{2,1,0:T(8,128)S(1)}, f32[2,48,128]{2,1,0:T(8,128)S(1)}, u32[]{:S(2)}, u32[]{:S(2)}) collective-permute-start(f32[2,48,128]{2,1,0:T(8,128)S(1)} %get-tuple-element.21), channel_id=1, source_target_pairs={{0,1},{16,19},{4,5},{20,23},{8,9},{24,27},{12,13},{28,31},{32,33},... | collective-permute-start | bytes 147464 | tf_op jit(solution)/shard_map/ppermute | solution.py:228
  69.1 4.9 %collective-permute-start.11 = (f32[1,48,128]{2,1,0:T(8,128)S(1)}, f32[1,48,128]{2,1,0:T(8,128)S(1)}, u32[]{:S(2)}, u32[]{:S(2)}) collective-permute-start(f32[1,48,128]{2,1,0:T(8,128)S(1)} %slice_add_fusion.8), channel_id=1, source_target_pairs={{0,8},{16,24},{4,12},{20,28},{8,0},{24,16},{12,4},{28,20},{32,40},... | collective-permute-start | bytes 73736 | tf_op jit(solution)/shard_map/ppermute | solution.py:250
